TPU v7x, 32 devices: a whole 2x2x4 slice. The times are simulated.
32 devices in a mesh: row: 4 (over x, core), col: 2 (over y), dp: 4 (over z).
Axes of the slice: x: 2, y: 2, z: 4, core: 2. Of those that a mesh axis runs over, the one named last changes fastest.
Arguments:
- tokens: bfloat16 [16384, 768], P(('dp', 'col', 'row')), may hold values from -6 to 6
- encoded: bfloat16 [12000, 768], P(('dp', 'col', 'row')), may hold values from -6 to 6
- branch: int32 [8, 4], P(('dp', 'col')), may hold values from 512 to 1024
- cotangent: bfloat16 [16384, 768], P(('dp', 'col', 'row')), may hold values from -6 to 6
- gain_self: float32 [768], replicated, may hold values from 0.5 to 1.5
- self_query: bfloat16 [768, 768], P('col', 'row'), may hold values from -0.21875 to 0.21875
- self_key: bfloat16 [768, 768], P('col', 'row'), may hold values from -0.21875 to 0.21875
- self_value: bfloat16 [768, 768], P('col', 'row'), may hold values from -0.21875 to 0.21875
- self_out: bfloat16 [768, 768], P('row', 'col'), may hold values from -3 to 3
- gain_cross: float32 [768], replicated, may hold values from 0.5 to 1.5
- cross_query: bfloat16 [768, 768], P('col', 'row'), may hold values from -0.21875 to 0.21875
- cross_key: bfloat16 [768, 768], P('col', 'row'), may hold values from -0.21875 to 0.21875
- cross_value: bfloat16 [768, 768], P('col', 'row'), may hold values from -0.21875 to 0.21875
- cross_out: bfloat16 [768, 768], P('row', 'col'), may hold values from -4 to 4
- gain_hidden: float32 [768], replicated, may hold values from 0.5 to 1.5
- hidden_up: bfloat16 [768, 3072], P('col', 'row'), may hold values from -0.21875 to 0.21875
- hidden_down: bfloat16 [3072, 768], P('row', 'col'), may hold values from -0.109375 to 0.109375
- gain_final: float32 [768], replicated, may hold values from 0.5 to 1.5
Outputs:
- layer_out: bfloat16 [16384, 768], P(('dp', 'col', 'row'))
- grad_tokens: float32 [16384, 768], P(('dp', 'col', 'row'))
- grad_encoded: float32 [12000, 768], P(('dp', 'col', 'row'))
- grad_gain_self: float32 [768], replicated
- grad_self_query: float32 [768, 768], P('col', 'row')
- grad_self_key: float32 [768, 768], P('col', 'row')
- grad_self_value: float32 [768, 768], P('col', 'row')
- grad_self_out: float32 [768, 768], P('row', 'col')
- grad_gain_cross: float32 [768], replicated
- grad_cross_query: float32 [768, 768], P('col', 'row')
- grad_cross_key: float32 [768, 768], P('col', 'row')
- grad_cross_value: float32 [768, 768], P('col', 'row')
- grad_cross_out: float32 [768, 768], P('row', 'col')
- grad_gain_hidden: float32 [768], replicated
- grad_hidden_up: float32 [768, 3072], P('col', 'row')
- grad_hidden_down: float32 [3072, 768], P('row', 'col')
- grad_gain_final: float32 [768], replicated
Inputs may be any that keep to these rules, and one draw needn't show every extreme that they name: Continuation j of family f sees the first branch[f, j] prompt positions.
All inputs are finite; a program needn't handle non-finite values.
Results may differ from a plain program's by a relative error of at most 0.025.
Values may be sent and summed in bfloat16 or wider, within the bound.
A program may use at most 192 MiB of HBM per device.

v0:
```python
import jax
import jax.numpy as jnp
from jax import lax
from jax.sharding import PartitionSpec as P

HEAD_DIM = 64
PROMPT = 1024
CONT = 256
NCONT = 4
eps = 1e-05
big_neg = -1e30


def matmul(left, right):
    return jnp.dot(left, right, preferred_element_type=jnp.float32)


def inner_left(left, right):
    return lax.dot_general(
        left, right, (((0,), (0,)), ((), ())), preferred_element_type=jnp.float32
    )


def inner_right(left, right):
    return lax.dot_general(
        left, right, (((1,), (1,)), ((), ())), preferred_element_type=jnp.float32
    )


def unit_rows(rows_in):
    average = jnp.mean(rows_in, axis=-1, keepdims=True)
    centred = rows_in - average
    variance = jnp.mean(centred * centred, axis=-1, keepdims=True)
    return centred * lax.rsqrt(variance + eps)


def norm_back(rows_in, gain, upstream):
    outcome, pullback = jax.vjp(lambda values_in: unit_rows(values_in) * gain, rows_in)
    return pullback(upstream)[0]


def visible(query_pos, key_pos, branch_row):
    query_at = query_pos[:, None]
    key_at = key_pos[None, :]
    query_cont = (query_at - PROMPT) // CONT
    key_cont = (key_at - PROMPT) // CONT
    chosen = (query_cont == jnp.arange(NCONT, dtype=jnp.int32)[None, :]).astype(jnp.int32)
    limit = jnp.sum(chosen * branch_row[None, :], axis=1, keepdims=True)
    same_cont = (key_cont == query_cont) & (key_at <= query_at)
    return jnp.where(
        query_at < PROMPT, key_at <= query_at, jnp.where(key_at < PROMPT, key_at < limit, same_cont)
    )


def block_scores(piece, split_k, anchor, key_pos, branch_row, scaling):
    scores = (
        jnp.einsum("qhd,khd->hqk", piece, split_k, preferred_element_type=jnp.float32) * scaling
    )
    if branch_row is not None:
        shown = visible(anchor + jnp.arange(piece.shape[0], dtype=jnp.int32), key_pos, branch_row)
        scores = jnp.where(shown[None], scores, big_neg)
    return scores


def attend(queries, key_rows, value_rows, branch_row):
    length = queries.shape[0]
    features = queries.shape[1]
    head_count = features // HEAD_DIM
    block_rows = min(512, length)
    blocks = length // block_rows
    scaling = HEAD_DIM ** (-0.5)
    split_q = queries.reshape(blocks, block_rows, head_count, HEAD_DIM)
    split_k = key_rows.reshape(key_rows.shape[0], head_count, HEAD_DIM)
    split_v = value_rows.reshape(value_rows.shape[0], head_count, HEAD_DIM)
    key_pos = jnp.arange(key_rows.shape[0], dtype=jnp.int32)

    def one_block(inputs):
        piece, anchor = inputs
        scores = block_scores(piece, split_k, anchor, key_pos, branch_row, scaling)
        highest = jnp.max(scores, axis=-1, keepdims=True)
        raised = jnp.exp(scores - highest)
        denominator = jnp.sum(raised, axis=-1, keepdims=True)
        weights = (raised / denominator).astype(jnp.bfloat16)
        blended = jnp.einsum("hqk,khd->qhd", weights, split_v, preferred_element_type=jnp.float32)
        return (
            blended.reshape(block_rows, features).astype(jnp.bfloat16),
            (highest + jnp.log(denominator))[..., 0],
        )

    starts = jnp.arange(blocks, dtype=jnp.int32) * block_rows
    blended, logsum = lax.map(one_block, (split_q, starts))
    return (blended.reshape(length, features), logsum)


def attend_back(queries, key_rows, value_rows, grad_blended, logsum, branch_row):
    length = queries.shape[0]
    features = queries.shape[1]
    head_count = features // HEAD_DIM
    block_rows = min(512, length)
    blocks = length // block_rows
    scaling = HEAD_DIM ** (-0.5)
    split_q = queries.reshape(blocks, block_rows, head_count, HEAD_DIM)
    split_g = grad_blended.reshape(blocks, block_rows, head_count, HEAD_DIM)
    split_k = key_rows.reshape(key_rows.shape[0], head_count, HEAD_DIM)
    split_v = value_rows.reshape(value_rows.shape[0], head_count, HEAD_DIM)
    key_pos = jnp.arange(key_rows.shape[0], dtype=jnp.int32)

    def one_block(running, inputs):
        piece, grad_piece, anchor, block_sum = inputs
        scores = block_scores(piece, split_k, anchor, key_pos, branch_row, scaling)
        weights = jnp.exp(scores - block_sum[..., None])
        rounded = weights.astype(jnp.bfloat16)
        through = jnp.einsum(
            "qhd,khd->hqk", grad_piece, split_v, preferred_element_type=jnp.float32
        )
        centre = jnp.sum(weights * through, axis=-1, keepdims=True)
        sloped = (weights * (through - centre)).astype(jnp.bfloat16)
        grad_query = (
            jnp.einsum("hqk,khd->qhd", sloped, split_k, preferred_element_type=jnp.float32)
            * scaling
        )
        grad_keys = (
            running[0]
            + jnp.einsum("hqk,qhd->khd", sloped, piece, preferred_element_type=jnp.float32)
            * scaling
        )
        grad_values = running[1] + jnp.einsum(
            "hqk,qhd->khd", rounded, grad_piece, preferred_element_type=jnp.float32
        )
        return ((grad_keys, grad_values), grad_query.reshape(block_rows, features))

    blank_keys = jnp.zeros((key_rows.shape[0], head_count, HEAD_DIM), jnp.float32)
    starts = jnp.arange(blocks, dtype=jnp.int32) * block_rows
    (grad_keys, grad_values), grad_query = lax.scan(
        one_block, (blank_keys, blank_keys), (split_q, split_g, starts, logsum)
    )
    return (
        grad_query.reshape(length, features).astype(jnp.bfloat16),
        grad_keys.reshape(-1, features).astype(jnp.bfloat16),
        grad_values.reshape(-1, features).astype(jnp.bfloat16),
    )


def local(
    tokens,
    encoded,
    branch,
    cotangent,
    gain_self,
    self_query,
    self_key,
    self_value,
    self_out,
    gain_cross,
    cross_query,
    cross_key,
    cross_value,
    cross_out,
    gain_hidden,
    hidden_up,
    hidden_down,
    gain_final,
):
    local_rows = tokens.shape[0]
    offset = lax.axis_index("row") * local_rows
    branch_row = branch[0]

    def spread(piece):
        return lax.all_gather(piece, "row", axis=0, tiled=True)

    def own_slice(value):
        return lax.dynamic_slice_in_dim(value, offset, local_rows, 0)

    def scatter_rows(parts, apply):
        return lax.psum_scatter(
            apply(tuple((piece for piece in parts))).astype(jnp.bfloat16),
            "row",
            scatter_dimension=0,
            tiled=True,
        ).astype(jnp.float32)

    def settle(parts, apply):
        return lax.psum(apply(parts), "row")

    def gain_term(upstream, rows_in):
        return jnp.sum(own_slice(upstream) * unit_rows(own_slice(rows_in)), axis=0)

    full_query, full_key, full_value, full_cquery, full_ckey, full_cvalue, full_up = (
        lax.all_gather(self_query, "col", axis=0, tiled=True),
        lax.all_gather(self_key, "col", axis=0, tiled=True),
        lax.all_gather(self_value, "col", axis=0, tiled=True),
        lax.all_gather(cross_query, "col", axis=0, tiled=True),
        lax.all_gather(cross_key, "col", axis=0, tiled=True),
        lax.all_gather(cross_value, "col", axis=0, tiled=True),
        lax.all_gather(hidden_up, "col", axis=0, tiled=True),
    )
    full_out, full_cout, full_down = (
        lax.all_gather(self_out, "col", axis=1, tiled=True),
        lax.all_gather(cross_out, "col", axis=1, tiled=True),
        lax.all_gather(hidden_down, "col", axis=1, tiled=True),
    )
    frames = spread(encoded)
    residual = spread(tokens).astype(jnp.float32)
    wide_self = (unit_rows(residual) * gain_self).astype(jnp.bfloat16)
    queries = matmul(wide_self, full_query).astype(jnp.bfloat16)
    key_rows = matmul(wide_self, full_key).astype(jnp.bfloat16)
    value_rows = matmul(wide_self, full_value).astype(jnp.bfloat16)
    blended_self, logsum_self = attend(queries, key_rows, value_rows, branch_row)
    after_self = residual + settle((blended_self,), lambda parts: matmul(parts[0], full_out))
    wide_cross = (unit_rows(after_self) * gain_cross).astype(jnp.bfloat16)
    cross_queries = matmul(wide_cross, full_cquery).astype(jnp.bfloat16)
    cross_keys = matmul(frames, full_ckey).astype(jnp.bfloat16)
    cross_values = matmul(frames, full_cvalue).astype(jnp.bfloat16)
    blended_cross, logsum_cross = attend(cross_queries, cross_keys, cross_values, None)
    after_cross = after_self + settle((blended_cross,), lambda parts: matmul(parts[0], full_cout))
    wide_hidden = (unit_rows(after_cross) * gain_hidden).astype(jnp.bfloat16)
    raised = matmul(wide_hidden, full_up)
    active = jax.nn.gelu(raised, approximate=False).astype(jnp.bfloat16)
    after_hidden = after_cross + settle((active,), lambda parts: matmul(parts[0], full_down))
    layer_out = own_slice(unit_rows(after_hidden) * gain_final).astype(jnp.bfloat16)
    upstream = spread(cotangent).astype(jnp.float32)
    final_gain = gain_term(upstream, after_hidden)
    grad_hidden = norm_back(after_hidden, gain_final, upstream)
    sent_hidden = grad_hidden.astype(jnp.bfloat16)
    grad_down = inner_left(active, sent_hidden)
    outcome, gelu_pull = jax.vjp(
        lambda values_in: jax.nn.gelu(values_in, approximate=False), raised
    )
    grad_raised = gelu_pull(inner_right(sent_hidden, full_down))[0].astype(jnp.bfloat16)
    grad_up = inner_left(wide_hidden, grad_raised)
    grad_normed = settle((grad_raised,), lambda parts: inner_right(parts[0], full_up))
    hidden_gain = gain_term(grad_normed, after_cross)
    grad_cross = grad_hidden + norm_back(after_cross, gain_hidden, grad_normed)
    sent_cross = grad_cross.astype(jnp.bfloat16)
    grad_cout = inner_left(blended_cross, sent_cross)
    grad_blended = inner_right(sent_cross, full_cout).astype(jnp.bfloat16)
    grad_cq, grad_ck, grad_cv = attend_back(
        cross_queries, cross_keys, cross_values, grad_blended, logsum_cross, None
    )
    grad_cquery = inner_left(wide_cross, grad_cq)
    grad_ckey = inner_left(frames, grad_ck)
    grad_cvalue = inner_left(frames, grad_cv)
    grad_encoded = scatter_rows(
        (grad_ck, grad_cv),
        lambda parts: inner_right(parts[0], full_ckey) + inner_right(parts[1], full_cvalue),
    )
    grad_normed = settle((grad_cq,), lambda parts: inner_right(parts[0], full_cquery))
    cross_gain = gain_term(grad_normed, after_self)
    grad_self = grad_cross + norm_back(after_self, gain_cross, grad_normed)
    sent_self = grad_self.astype(jnp.bfloat16)
    grad_out = inner_left(blended_self, sent_self)
    grad_blended = inner_right(sent_self, full_out).astype(jnp.bfloat16)
    grad_qs, grad_ks, grad_vs = attend_back(
        queries, key_rows, value_rows, grad_blended, logsum_self, branch_row
    )
    grad_query = inner_left(wide_self, grad_qs)
    grad_key = inner_left(wide_self, grad_ks)
    grad_value = inner_left(wide_self, grad_vs)
    grad_normed = settle(
        (grad_qs, grad_ks, grad_vs),
        lambda parts: inner_right(parts[0], full_query)
        + inner_right(parts[1], full_key)
        + inner_right(parts[2], full_value),
    )
    self_gain = gain_term(grad_normed, residual)
    grad_tokens = own_slice(grad_self + norm_back(residual, gain_self, grad_normed))
    grad_query, grad_key, grad_value, grad_cquery, grad_ckey, grad_cvalue, grad_up = (
        lax.psum_scatter(
            grad_query.astype(jnp.bfloat16), "col", scatter_dimension=0, tiled=True
        ).astype(jnp.float32),
        lax.psum_scatter(
            grad_key.astype(jnp.bfloat16), "col", scatter_dimension=0, tiled=True
        ).astype(jnp.float32),
        lax.psum_scatter(
            grad_value.astype(jnp.bfloat16), "col", scatter_dimension=0, tiled=True
        ).astype(jnp.float32),
        lax.psum_scatter(
            grad_cquery.astype(jnp.bfloat16), "col", scatter_dimension=0, tiled=True
        ).astype(jnp.float32),
        lax.psum_scatter(
            grad_ckey.astype(jnp.bfloat16), "col", scatter_dimension=0, tiled=True
        ).astype(jnp.float32),
        lax.psum_scatter(
            grad_cvalue.astype(jnp.bfloat16), "col", scatter_dimension=0, tiled=True
        ).astype(jnp.float32),
        lax.psum_scatter(
            grad_up.astype(jnp.bfloat16), "col", scatter_dimension=0, tiled=True
        ).astype(jnp.float32),
    )
    grad_out, grad_cout, grad_down = (
        lax.psum_scatter(
            grad_out.astype(jnp.bfloat16), "col", scatter_dimension=1, tiled=True
        ).astype(jnp.float32),
        lax.psum_scatter(
            grad_cout.astype(jnp.bfloat16), "col", scatter_dimension=1, tiled=True
        ).astype(jnp.float32),
        lax.psum_scatter(
            grad_down.astype(jnp.bfloat16), "col", scatter_dimension=1, tiled=True
        ).astype(jnp.float32),
    )
    summed = (
        lax.psum(grad_query.astype(jnp.bfloat16), "dp").astype(jnp.float32),
        lax.psum(grad_key.astype(jnp.bfloat16), "dp").astype(jnp.float32),
        lax.psum(grad_value.astype(jnp.bfloat16), "dp").astype(jnp.float32),
        lax.psum(grad_out.astype(jnp.bfloat16), "dp").astype(jnp.float32),
        lax.psum(grad_cquery.astype(jnp.bfloat16), "dp").astype(jnp.float32),
        lax.psum(grad_ckey.astype(jnp.bfloat16), "dp").astype(jnp.float32),
        lax.psum(grad_cvalue.astype(jnp.bfloat16), "dp").astype(jnp.float32),
        lax.psum(grad_cout.astype(jnp.bfloat16), "dp").astype(jnp.float32),
        lax.psum(grad_up.astype(jnp.bfloat16), "dp").astype(jnp.float32),
        lax.psum(grad_down.astype(jnp.bfloat16), "dp").astype(jnp.float32),
    )
    gains = lax.psum((self_gain, cross_gain, hidden_gain, final_gain), ("row", "col", "dp"))
    return (
        layer_out,
        grad_tokens,
        grad_encoded,
        gains[0],
        summed[0],
        summed[1],
        summed[2],
        summed[3],
        gains[1],
        summed[4],
        summed[5],
        summed[6],
        summed[7],
        gains[2],
        summed[8],
        summed[9],
        gains[3],
    )


def solution(mesh):
    return jax.shard_map(
        local,
        mesh=mesh,
        in_specs=(
            P(("dp", "col", "row"), None),
            P(("dp", "col", "row"), None),
            P(("dp", "col"), None),
            P(("dp", "col", "row"), None),
            P(),
            P("col", "row"),
            P("col", "row"),
            P("col", "row"),
            P("row", "col"),
            P(),
            P("col", "row"),
            P("col", "row"),
            P("col", "row"),
            P("row", "col"),
            P(),
            P("col", "row"),
            P("row", "col"),
            P(),
        ),
        out_specs=(
            P(("dp", "col", "row"), None),
            P(("dp", "col", "row"), None),
            P(("dp", "col", "row"), None),
            P(),
            P("col", "row"),
            P("col", "row"),
            P("col", "row"),
            P("row", "col"),
            P(),
            P("col", "row"),
            P("col", "row"),
            P("col", "row"),
            P("row", "col"),
            P(),
            P("col", "row"),
            P("row", "col"),
            P(),
        ),
        check_vma=False,
    )
```

profile of v0, /device:TPU:0, one launch (start us, length us, event | category | flops | bytes accessed | tf_op | source)
XLA Modules:
  0.0 1545.6 jit_solution(5854435203476800310)
XLA Ops:
  9.6 7.8 all_gather.40
  17.3 6.0 all_gather.41
  23.4 6.0 all_gather.42
  29.4 6.0 all_gather.43
  35.4 6.3 all-gather.7.cloned.1.call-done
  55.5 94.7 %while.64 = (s32[]{:T(128)}, bf16[4,512,192]{1,2,0:T(8,128)(2,1)S(1)}, f32[4,3,512]{2,1,0:T(4,128)S(1)}, s32[4]{0:T(128)S(1)}, s32[1,4]{1,0:T(1,128)S(1)}, /*ind...) while((s32[]{:T(128)}, ...), condition=%wide.region_6.7_spmd.clone.clone, body=%wide.region_2.6_spmd.clone.clone.sunk | while | flops 849493504 | bytes 44393620 | solution.py:91
  59.7 6.0 fusion.265
  65.8 6.8 fusion.266
  72.6 6.7 fusion.267
  83.5 6.0 fusion.265
  89.5 6.8 fusion.266
  96.2 6.7 fusion.267
  107.1 6.0 fusion.265
  113.1 6.8 fusion.266
  119.9 6.7 fusion.267
  130.8 6.0 fusion.265
  136.8 6.8 fusion.266
  143.6 6.7 fusion.267
  155.3 6.7 all_gather.44
  162.0 5.8 all_gather.46
  167.8 5.8 all_gather.47
  173.6 6.0 all_gather.48
  188.5 86.4 %all-reduce.12.cloned.1.call-done = f32[2048,768]{1,0:T(8,128)} async-done(((f32[2048,768]{1,0:T(8,128)}), f32[2048,768]{1,0:T(8,128)}) %all-reduce.12.cloned.1.call-update) | async-done | bytes 6291472 | tf_op jit(solution)/shard_map/psum | solution.py:183
  288.2 20.2 %while.63 = (s32[]{:T(128)}, bf16[4,512,192]{1,2,0:T(8,128)(2,1)S(1)}, f32[4,3,512]{2,1,0:T(4,128)S(1)}, bf16[4,512,3,64]{1,3,2,0:T(8,128)(2,1)S(1)}, bf16[1500,...) while((s32[]{:T(128)}, bf16[4,512,192]{1,2,0:T(8,128)(2,1)S(1)}, ...), condition=%wide.region_13.14_spmd, body=%wide.region_10.13_spmd.sunk | while | flops 610656768 | bytes 29655648 | solution.py:91
  314.9 118.3 %all-reduce.14.cloned.1.call-done = f32[2048,768]{1,0:T(8,128)} async-done(((f32[2048,768]{1,0:T(8,128)}), f32[2048,768]{1,0:T(8,128)}) %all-reduce.14.cloned.1.call-update) | async-done | bytes 6291472 | tf_op jit(solution)/shard_map/psum | solution.py:183
  433.2 5.3 fusion.142
  443.5 18.7 %multiply_convert_fusion.2 = (bf16[2048,768]{1,0:T(8,128)(2,1)}, f32[2048,768]{1,0:T(8,128)}, f32[2048,768]{1,0:T(8,128)}) fusion(bf16[2048,768]{1,0:T(8,128)(2,1)} %multiply_convert_fusion.3, bf16[768,768]{1,0:T(8,128)(2,1)} %all-gather.9.cloned.1.call-done), kind=kOutput, calls=%fused_computation.165 | convolution fusion | flops 2518155264 | bytes 20054016 | tf_op jit(solution)/shard_map/dot_general | solution.py:15
  462.1 7.5 fusion.146
  470.5 119.1 %all-reduce.16.cloned.1.call-done = f32[2048,768]{1,0:T(8,128)} async-done(((f32[2048,768]{1,0:T(8,128)}), f32[2048,768]{1,0:T(8,128)}) %all-reduce.16.cloned.1.call-update) | async-done | bytes 6291472 | tf_op jit(solution)/shard_map/psum | solution.py:183
  589.6 7.9 fusion.140
  597.5 22.3 %all-gather.13.cloned.1.call-done = bf16[2048,768]{1,0:T(8,128)(2,1)} async-done(((bf16[512,768]{1,0:T(8,128)(2,1)}), bf16[2048,768]{1,0:T(8,128)(2,1)}) %all-gather.13.cloned.1.call-update) | async-done | bytes 3145744 | tf_op jit(solution)/shard_map/all_gather | solution.py:169
  643.9 119.7 %all-reduce.18.cloned.1.call-done = f32[2048,768]{1,0:T(8,128)} async-done(((f32[2048,768]{1,0:T(8,128)}), f32[2048,768]{1,0:T(8,128)}) %all-reduce.18.cloned.1.call-update) | async-done | bytes 6291472 | tf_op jit(solution)/shard_map/psum | solution.py:183
  763.6 5.5 multiply_reduce_fusion.5
  786.2 110.7 %while.65 = (s32[]{:T(128)}, f32[1500,3,64]{0,2,1:T(8,128)S(1)}, f32[1500,3,64]{0,2,1:T(8,128)S(1)}, bf16[4,512,192]{1,2,0:T(8,128)(2,1)}, bf16[4,512,3,64]{1,3,...) while((s32[]{:T(128)}, f32[1500,3,64]{0,2,1:T(8,128)S(1)}, ...), condition=%wide.region_27.28_spmd.clone, body=%wide.region_25.27_spmd.clone.sunk | while | flops 1503843072 | bytes 135411952 | solution.py:134
  796.2 10.9 multiply_convert_fusion.8
  823.8 10.9 multiply_convert_fusion.8
  851.4 10.9 multiply_convert_fusion.8
  879.0 10.9 multiply_convert_fusion.8
  903.7 7.6 convolution_convert_fusion.8
  931.7 91.9 %all-reduce.20.cloned.1.call-done = f32[2048,768]{1,0:T(8,128)} async-done(((f32[2048,768]{1,0:T(8,128)}), f32[2048,768]{1,0:T(8,128)}) %all-reduce.20.cloned.1.call-update) | async-done | bytes 6291472 | tf_op jit(solution)/shard_map/psum | solution.py:183
  1023.6 5.5 multiply_reduce_fusion.4
  1030.0 6.1 fusion.137
  1050.2 141.9 %while.66 = (s32[]{:T(128)}, f32[2048,3,64]{0,2,1:T(8,128)}, f32[2048,3,64]{0,2,1:T(8,128)}, bf16[4,512,192]{1,2,0:T(8,128)(2,1)}, bf16[4,512,3,64]{1,3,2,0:T(8,...) while((s32[]{:T(128)}, f32[2048,3,64]{0,2,1:T(8,128)}, ...), condition=%wide.region_34.35_spmd.clone.clone, body=%wide.region_31.34_spmd.clone.clone.sunk | while | flops 2068954624 | bytes 147471712 | solution.py:134
  1063.1 5.8 multiply_reduce_fusion.24
  1068.9 6.1 multiply_convert_fusion.9
  1075.0 5.1 convolution_multiply_fusion.7
  1092.3 6.1 fusion.293
  1098.4 5.8 multiply_reduce_fusion.24
  1104.2 6.1 multiply_convert_fusion.9
  1110.3 5.1 convolution_multiply_fusion.7
  1128.2 6.1 fusion.293
  1134.3 5.8 multiply_reduce_fusion.24
  1140.1 6.1 multiply_convert_fusion.9
  1146.2 5.1 convolution_multiply_fusion.7
  1164.1 6.1 fusion.293
  1170.2 5.8 multiply_reduce_fusion.24
  1175.9 6.1 multiply_convert_fusion.9
  1207.5 6.6 convolution_convert_fusion.9
  1216.0 8.2 convert_element_type.265
  1244.0 22.8 %reduce-scatter.31.cloned.1.call-done = bf16[384,768]{1,0:T(8,128)(2,1)} async-done(((bf16[768,768]{1,0:T(8,128)(2,1)}), bf16[384,768]{1,0:T(8,128)(2,1)}) %reduce-scatter.31.cloned.1.call-update) | async-done | bytes 589840 | tf_op jit(solution)/shard_map/reduce_scatter | solution.py:286
  1288.5 25.8 %fusion.4 = bf16[376,768]{1,0:T(8,128)(2,1)} fusion(bf16[1500,768]{1,0:T(8,128)(2,1)} %add_convert_fusion.2), kind=kCustom, calls=%all-reduce-scatter | all-reduce-scatter fusion | flops 1155073 | bytes 2882048
  1327.8 37.6 %all-reduce.24.cloned.1.call-done = (bf16[384,192]{0,1:T(8,128)(2,1)}, bf16[384,192]{0,1:T(8,128)(2,1)}, bf16[384,192]{0,1:T(8,128)(2,1)}, bf16[192,384]{1,0:T(8...) async-done(((bf16[384,192]{0,1:T(8,128)(2,1)}, ...) | async-done | bytes 2359312 | tf_op jit(solution)/shard_map/psum | solution.py:302
  1382.9 103.1 %all-reduce.22.cloned.1.call-done = f32[2048,768]{1,0:T(8,128)} async-done(((f32[2048,768]{1,0:T(8,128)}), f32[2048,768]{1,0:T(8,128)}) %all-reduce.22.cloned.1.call-update) | async-done | bytes 6291472 | tf_op jit(solution)/shard_map/psum | solution.py:183
  1498.0 39.8 %all-reduce.2 = (f32[768]{0:T(1024)}, f32[768]{0:T(1024)}, f32[768]{0:T(1024)}, f32[768]{0:T(1024)}) all-reduce(f32[768]{0:T(1024)S(1)} %multiply_reduce_fusion.17, f32[768]{0:T(1024)S(1)} %multiply_reduce_fusion.15, f32[768]{0:T(1024)S(1)} %multiply_reduce_fusion.13, ...), channel_id=1, replica_groups=mesh['row'=4,'col'=2,'dp'=4] {'row','col','dp'}, use_global_device_ids=true, to_apply=%region_42.43 | all-reduce | flops 3072 | bytes 24576 | tf_op jit(solution)/shard_map/psum | solution.py:313
  (602 shorter events, 401.3 us)
Async XLA Ops:
  8.0 39.2 %copy-start.82 = (f32[768]{0:T(1024)S(1)}, f32[768]{0:T(1024)}, u32[]{:S(2)}) copy-start(f32[768]{0:T(1024)} %param.30) | copy-start | bytes 9220
  8.0 33.6 %all-gather.7.cloned.1.call-start = ((), (), s32[]{:S(2)}) async-start(), calls=%async_computation.10 | async-start | bytes 3932160 | tf_op jit(solution)/shard_map/all_gather | solution.py:169
  8.8 170.9 %all-gather.15.cloned.1.call-start = ((), (), s32[]{:S(2)}) async-start(), calls=%async_computation.21 | async-start | bytes 2887680 | tf_op jit(solution)/shard_map/all_gather | solution.py:169
  9.5 265.4 %all-reduce.12.cloned.1.call-start = ((), (), s32[]{:S(2)}) async-start(), calls=%async_computation.11 | async-start | bytes 12582912 | tf_op jit(solution)/shard_map/psum | solution.py:183
  17.3 33.6 %copy-start.48 = (bf16[768,192]{0,1:T(8,128)(2,1)}, bf16[768,192]{0,1:T(8,128)(2,1)S(1)}, u32[]{:S(2)}) copy-start(bf16[768,192]{0,1:T(8,128)(2,1)S(1)} %all_gather.40) | copy-start | bytes 884740
  23.4 26.3 %copy-start.50 = (bf16[768,192]{0,1:T(8,128)(2,1)}, bf16[768,192]{0,1:T(8,128)(2,1)S(1)}, u32[]{:S(2)}) copy-start(bf16[768,192]{0,1:T(8,128)(2,1)S(1)} %all_gather.41) | copy-start | bytes 884740
  29.4 19.1 %copy-start.55 = (bf16[768,192]{0,1:T(8,128)(2,1)}, bf16[768,192]{0,1:T(8,128)(2,1)S(1)}, u32[]{:S(2)}) copy-start(bf16[768,192]{0,1:T(8,128)(2,1)S(1)} %all_gather.42) | copy-start | bytes 884740
  35.4 115.0 %copy-start.43 = (bf16[192,768]{1,0:T(8,128)(2,1)}, bf16[192,768]{1,0:T(8,128)(2,1)S(1)}, u32[]{:S(2)}) copy-start(bf16[192,768]{1,0:T(8,128)(2,1)S(1)} %all_gather.43) | copy-start | bytes 884740
  150.3 29.3 %copy-start.37 = (bf16[4,512,3,64]{1,3,2,0:T(8,128)(2,1)}, bf16[4,512,3,64]{1,3,2,0:T(8,128)(2,1)S(1)}, u32[]{:S(2)}) copy-start(bf16[4,512,3,64]{1,3,2,0:T(8,128)(2,1)S(1)} %get-tuple-element.1281) | copy-start | bytes 2359300
  150.3 129.0 %copy-start.64 = (f32[4,3,512]{2,1,0:T(4,128)}, f32[4,3,512]{2,1,0:T(4,128)S(1)}, u32[]{:S(2)}) copy-start(f32[4,3,512]{2,1,0:T(4,128)S(1)} %get-tuple-element.1177) | copy-start | bytes 73732
  151.4 10.6 copy-start.66
  155.1 12.7 copy-start.67
  155.1 18.5 %copy-start.68 = (bf16[192,384]{1,0:T(8,128)(2,1)S(1)}, bf16[192,384]{1,0:T(8,128)(2,1)}, u32[]{:S(2)}) copy-start(bf16[192,384]{1,0:T(8,128)(2,1)} %param.39) | copy-start | bytes 442372
  155.2 278.0 %all-reduce.14.cloned.1.call-start = ((), (), s32[]{:S(2)}) async-start(), calls=%async_computation.12 | async-start | bytes 12582912 | tf_op jit(solution)/shard_map/psum | solution.py:183
  162.0 119.2 %copy-start.54 = (bf16[768,192]{0,1:T(8,128)(2,1)}, bf16[768,192]{0,1:T(8,128)(2,1)S(1)}, u32[]{:S(2)}) copy-start(bf16[768,192]{0,1:T(8,128)(2,1)S(1)} %all_gather.44) | copy-start | bytes 884740
  167.8 20.7 %copy-start.52 = (bf16[768,192]{0,1:T(8,128)(2,1)}, bf16[768,192]{0,1:T(8,128)(2,1)S(1)}, u32[]{:S(2)}) copy-start(bf16[768,192]{0,1:T(8,128)(2,1)S(1)} %all_gather.46) | copy-start | bytes 884740
  173.6 14.9 copy-start.57
  179.6 128.9 %copy-start.45 = (bf16[192,768]{1,0:T(8,128)(2,1)}, bf16[192,768]{1,0:T(8,128)(2,1)S(1)}, u32[]{:S(2)}) copy-start(bf16[192,768]{1,0:T(8,128)(2,1)S(1)} %all_gather.48) | copy-start | bytes 884740
  313.3 130.2 %all-gather.9.cloned.1.call-start = ((), (), s32[]{:S(2)}) async-start(), calls=%async_computation.13 | async-start | bytes 1769472 | tf_op jit(solution)/shard_map/all_gather | solution.py:195
  313.9 148.3 %all-gather.11.cloned.1.call-start = ((), (), s32[]{:S(2)}) async-start(), calls=%async_computation.14 | async-start | bytes 1769472 | tf_op jit(solution)/shard_map/all_gather | solution.py:200
  314.5 275.1 %all-reduce.16.cloned.1.call-start = ((), (), s32[]{:S(2)}) async-start(), calls=%async_computation.15 | async-start | bytes 12582912 | tf_op jit(solution)/shard_map/psum | solution.py:183
  469.6 150.1 %all-gather.13.cloned.1.call-start = ((), (), s32[]{:S(2)}) async-start(), calls=%async_computation.16 | async-start | bytes 3932160 | tf_op jit(solution)/shard_map/all_gather | solution.py:169
  470.2 149.5 %copy-start.80 = (f32[768]{0:T(1024)S(1)}, f32[768]{0:T(1024)}, u32[]{:S(2)}) copy-start(f32[768]{0:T(1024)} %param.43) | copy-start | bytes 9220
  470.2 293.3 %all-reduce.18.cloned.1.call-start = ((), (), s32[]{:S(2)}) async-start(), calls=%async_computation.17 | async-start | bytes 12582912 | tf_op jit(solution)/shard_map/psum | solution.py:183
  619.8 8.1 slice-start.10
  619.8 10.1 slice-start.12
  624.6 8.2 slice-start.13
  624.7 8.4 copy-start.91
  627.8 9.8 copy-start.22
  627.8 146.6 %copy-start.87 = (f32[2048]{0:T(1024)}, f32[2048]{0:T(1024)S(1)}, u32[]{:S(2)}) copy-start(f32[2048]{0:T(1024)S(1)} %negate_multiply_fusion.4) | copy-start | bytes 24580
  643.8 379.8 %all-reduce.20.cloned.1.call-start = ((), (), s32[]{:S(2)}) async-start(), calls=%async_computation.18 | async-start | bytes 12582912 | tf_op jit(solution)/shard_map/psum | solution.py:183
  763.6 10.9 slice-start.8
  778.0 8.2 copy-start.26
  903.6 324.5 %reduce-scatter.49.cloned.1.call-start = ((), (), s32[]{:S(2)}) async-start(), calls=%async_computation.30 | async-start | bytes 1769472
  914.0 316.3 %reduce-scatter.47.cloned.1.call-start = ((), (), s32[]{:S(2)}) async-start(), calls=%async_computation.29 | async-start | bytes 589824
  918.9 313.1 %reduce-scatter.41.cloned.1.call-start = ((), (), s32[]{:S(2)}) async-start(), calls=%async_computation.26 | async-start | bytes 589824
  923.2 310.5 %reduce-scatter.43.cloned.1.call-start = ((), (), s32[]{:S(2)}) async-start(), calls=%async_computation.27 | async-start | bytes 589824
  923.3 100.3 %copy-start.62 = (f32[2048]{0:T(1024)S(1)}, f32[2048]{0:T(1024)}, u32[]{:S(2)}) copy-start(f32[2048]{0:T(1024)} %copy-done.61) | copy-start | bytes 24580
  923.4 100.2 %copy-start.86 = (f32[768]{0:T(1024)S(1)}, f32[768]{0:T(1024)}, u32[]{:S(2)}) copy-start(f32[768]{0:T(1024)} %param.35) | copy-start | bytes 9220
  927.4 308.0 %reduce-scatter.45.cloned.1.call-start = ((), (), s32[]{:S(2)}) async-start(), calls=%async_computation.28 | async-start | bytes 589824
  931.6 97.5 %copy-start.74 = (f32[2048]{0:T(1024)S(1)}, f32[2048]{0:T(1024)}, u32[]{:S(2)}) copy-start(f32[2048]{0:T(1024)} %copy-done.73) | copy-start | bytes 24580
  931.6 97.5 %copy-start.76 = (f32[2048]{0:T(1024)S(1)}, f32[2048]{0:T(1024)}, u32[]{:S(2)}) copy-start(f32[2048]{0:T(1024)} %copy-done.75) | copy-start | bytes 24580
  931.7 305.5 %reduce-scatter.39.cloned.1.call-start = ((), (), s32[]{:S(2)}) async-start(), calls=%async_computation.25 | async-start | bytes 589824
  1023.6 12.5 slice-start.4
  1049.2 189.6 %reduce-scatter.33.cloned.1.call-start = ((), (), s32[]{:S(2)}) async-start(), calls=%async_computation.22 | async-start | bytes 589824
  1198.0 42.5 %reduce-scatter.35.cloned.1.call-start = ((), (), s32[]{:S(2)}) async-start(), calls=%async_computation.23 | async-start | bytes 589824
  1203.1 39.2 %reduce-scatter.37.cloned.1.call-start = ((), (), s32[]{:S(2)}) async-start(), calls=%async_computation.24 | async-start | bytes 589824
  1206.5 9.0 copy-start.7
  1207.4 59.4 %reduce-scatter.31.cloned.1.call-start = ((), (), s32[]{:S(2)}) async-start(), calls=%async_computation.20 | async-start | bytes 1769472 | tf_op jit(solution)/shard_map/reduce_scatter | solution.py:286
  1214.1 151.3 %all-reduce.24.cloned.1.call-start = ((), (), s32[]{:S(2)}) async-start(), calls=%async_computation.31 | async-start | bytes 4718592 | tf_op jit(solution)/shard_map/psum | solution.py:302
  1215.4 9.2 slice-start
  1215.5 9.7 slice-start.2
  1216.0 8.7 copy-start.23
  1216.0 8.8 slice-start.1
  1216.0 9.7 slice-start.3
  1216.0 10.9 slice-start.6
  1227.6 42.4 %copy-start.81 = (f32[768]{0:T(1024)S(1)}, f32[768]{0:T(1024)}, u32[]{:S(2)}) copy-start(f32[768]{0:T(1024)} %param.43) | copy-start | bytes 9220
  1228.1 44.6 %copy-start.53 = (bf16[768,192]{0,1:T(8,128)(2,1)S(1)}, bf16[768,192]{0,1:T(8,128)(2,1)}, u32[]{:S(2)}) copy-start(bf16[768,192]{0,1:T(8,128)(2,1)} %copy-done.52) | copy-start | bytes 884740
  1266.8 219.2 %all-reduce.22.cloned.1.call-start = ((), (), s32[]{:S(2)}) async-start(), calls=%async_computation.19 | async-start | bytes 12582912 | tf_op jit(solution)/shard_map/psum | solution.py:183
  1315.0 3.5 collective-permute-start
  1318.4 167.6 %copy-start.60 = (f32[2048]{0:T(1024)S(1)}, f32[2048]{0:T(1024)}, u32[]{:S(2)}) copy-start(f32[2048]{0:T(1024)} %copy-done.59) | copy-start | bytes 24580
  1318.5 167.6 %copy-start.83 = (f32[768]{0:T(1024)S(1)}, f32[768]{0:T(1024)}, u32[]{:S(2)}) copy-start(f32[768]{0:T(1024)} %param.30) | copy-start | bytes 9220
  1378.6 111.3 %copy-start.72 = (f32[2048]{0:T(1024)S(1)}, f32[2048]{0:T(1024)}, u32[]{:S(2)}) copy-start(f32[2048]{0:T(1024)} %copy-done.71) | copy-start | bytes 24580
  1378.6 111.3 %copy-start.70 = (f32[2048]{0:T(1024)S(1)}, f32[2048]{0:T(1024)}, u32[]{:S(2)}) copy-start(f32[2048]{0:T(1024)} %copy-done.69) | copy-start | bytes 24580
  (92 other events, 380.2 us)
Sparse Core Ops, SparseCore 0:
  10.4 31.2 all-gather.6
  43.2 23.7 all-gather.14
  155.3 119.5 all-reduce.11
  313.4 119.7 all-reduce.13
  469.8 119.7 all-reduce.15
  591.0 28.7 all-gather.12
  643.9 119.5 all-reduce.17
  903.8 119.7 all-reduce.19
Sparse Core Ops, SparseCore 1:
  315.3 22.8 all-gather.8
  339.6 22.6 all-gather.10
  914.1 22.0 reduce-scatter.48
  938.4 13.1 reduce-scatter.46
  953.9 13.1 reduce-scatter.40
  969.3 13.1 reduce-scatter.42
  984.6 13.1 reduce-scatter.44
  1049.3 13.3 reduce-scatter.38
  1198.1 13.3 reduce-scatter.32
  1213.8 13.1 reduce-scatter.34
  1229.0 13.1 reduce-scatter.36
  1245.0 21.7 reduce-scatter.30
  1270.5 94.9 all-reduce.23
  1367.8 118.2 all-reduce.21
where the time goes:
time: 1550 us
  waiting for transfers between devices  731 us (47%)
  matrix products  331 us (21%)
  other arithmetic  244 us (16%)
  blocking collectives  116 us (7%)
  local copies, waits for them, and re-layouts  101 us (7%)
  between operations  18.4 us (1%)
    psum x6, waiting for transfers between devices, settle(): return lax.psum(apply(parts), 'row')  638 us
    unnamed x227, local copies, waits for them, and re-layouts  69.1 us
    convert_element_type x8, other arithmetic, one_block(): sloped = (weights * (through - centre)).astype(jnp.bfloat16)  68 us
    dot_general x16, matrix products, block_scores(): jnp.einsum('qhd,khd->hqk', piece, split_k, preferred_element_type=jnp.flo...  51.3 us
    dot_general x10, matrix products, matmul(): return jnp.dot(left, right, preferred_element_type=jnp.float32)  45.2 us
    dot_general x8, matrix products, one_block(): jnp.einsum('qhd,khd->hqk', grad_piece, split_v, preferred_element_type=jn...  42.6 us
    psum x1, blocking collectives, local(): lax.psum((self_gain, cross_gain, hidden_gain, final_gain), ('row', 'col',...  39.8 us
    psum x1, waiting for transfers between devices, local(): lax.psum(grad_query.astype(jnp.bfloat16), 'dp').astype(jnp.float32)  37.6 us
  transfers between devices with their start and end apart: 23, of which 10 were waited for; matrix products, arithmetic and copies ran while one was open for 30% of the time, Pallas kernels for 0%

commit v1 on v0

--- a/solution.py
+++ b/solution.py
@@ -180,7 +180,7 @@
         ).astype(jnp.float32)
 
     def settle(parts, apply):
-        return lax.psum(apply(parts), "row")
+        return lax.all_gather(apply(parts), "row").sum(axis=0)
 
     def gain_term(upstream, rows_in):
         return jnp.sum(own_slice(upstream) * unit_rows(own_slice(rows_in)), axis=0)

time: 1550 us -> 1840 us (1.19)
  waiting for transfers between devices: 731 us -> 940 us
  other arithmetic: 244 us -> 320 us
    all_gather x0 -> x6, waiting for transfers between devices: none -> 845 us  [settle(): return lax.all_gather(apply(parts), 'row').sum(axis=0)]
    psum x6 -> x0, waiting for transfers between devices: 638 us -> none  [settle(): return lax.psum(apply(parts), 'row')]
    reduce_sum x0 -> x6, other arithmetic: none -> 76.8 us  [settle(): return lax.all_gather(apply(parts), 'row').sum(axis=0)]
    unnamed x227 -> x235, local copies, waits for them, and re-layouts: 69.1 us -> 63.4 us
  transfers between devices with their start and end apart: 23 -> 23, of which waited for: 10 -> 13; matrix products, arithmetic and copies ran while one was open for 30% -> 28% of each run, Pallas kernels for 0% -> 0%
where the time goes in v1:
time: 1840 us; the launch traced here: 1820 us
  waiting for transfers between devices  940 us (51%)
  matrix products  331 us (18%)
  other arithmetic  320 us (17%)
  blocking collectives  115 us (6%)
  local copies, waits for them, and re-layouts  95.5 us (5%)
    all_gather x6, waiting for transfers between devices, settle(): return lax.all_gather(apply(parts), 'row').sum(axis=0)  845 us
    reduce_sum x6, other arithmetic, settle(): return lax.all_gather(apply(parts), 'row').sum(axis=0)  76.8 us
    convert_element_type x8, other arithmetic, one_block(): sloped = (weights * (through - centre)).astype(jnp.bfloat16)  68.4 us
    unnamed x235, local copies, waits for them, and re-layouts  63.4 us
    dot_general x16, matrix products, block_scores(): jnp.einsum('qhd,khd->hqk', piece, split_k, preferred_element_type=jnp.flo...  51.3 us
    dot_general x10, matrix products, matmul(): return jnp.dot(left, right, preferred_element_type=jnp.float32)  45.9 us
    dot_general x8, matrix products, one_block(): jnp.einsum('qhd,khd->hqk', grad_piece, split_v, preferred_element_type=jn...  42.6 us
    psum x1, blocking collectives, local(): lax.psum((self_gain, cross_gain, hidden_gain, final_gain), ('row', 'col',...  39.5 us
  transfers between devices with their start and end apart: 23, of which 13 were waited for; matrix products, arithmetic and copies ran while one was open for 28% of the time, Pallas kernels for 0%

profile of v1, /device:TPU:0, one launch (start us, length us, event | category | flops | bytes accessed | tf_op | source)
XLA Modules:
  0.0 1824.0 jit_solution(8895228092244819178)
XLA Ops:
  8.7 7.8 all_gather.76
  16.5 6.0 all_gather.77
  22.5 6.0 all_gather.78
  28.5 6.0 all_gather.79
  34.6 6.3 all-gather.19.cloned.1.call-done
  54.5 94.8 %while.64 = (s32[]{:T(128)}, bf16[4,512,192]{1,2,0:T(8,128)(2,1)S(1)}, f32[4,3,512]{2,1,0:T(4,128)S(1)}, s32[4]{0:T(128)S(1)}, s32[1,4]{1,0:T(1,128)S(1)}, /*ind...) while((s32[]{:T(128)}, ...), condition=%wide.region_6.7_spmd.clone.clone, body=%wide.region_2.6_spmd.clone.clone.sunk | while | flops 849493504 | bytes 44393620 | solution.py:91
  58.7 6.1 fusion.265
  64.8 6.8 fusion.266
  71.5 6.7 fusion.267
  82.4 6.0 fusion.265
  88.5 6.8 fusion.266
  95.2 6.7 fusion.267
  106.1 6.0 fusion.265
  112.1 6.8 fusion.266
  118.9 6.7 fusion.267
  129.8 6.0 fusion.265
  135.8 6.8 fusion.266
  142.6 6.7 fusion.267
  154.3 6.7 all_gather.82
  161.1 5.8 all_gather.84
  166.9 5.8 all_gather.85
  172.7 6.0 all_gather.86
  187.5 121.7 %all-gather.27.cloned.1.call-done = f32[8192,768]{1,0:T(8,128)} async-done(((f32[2048,768]{1,0:T(8,128)}), f32[8192,768]{1,0:T(8,128)}) %all-gather.27.cloned.1.call-update) | async-done | bytes 25165840 | tf_op jit(solution)/shard_map/all_gather | solution.py:183
  309.2 12.7 reduce_sum.386
  335.3 20.2 %while.63 = (s32[]{:T(128)}, bf16[4,512,192]{1,2,0:T(8,128)(2,1)S(1)}, f32[4,3,512]{2,1,0:T(4,128)S(1)}, bf16[4,512,3,64]{1,3,2,0:T(8,128)(2,1)S(1)}, bf16[1500,...) while((s32[]{:T(128)}, bf16[4,512,192]{1,2,0:T(8,128)(2,1)S(1)}, ...), condition=%wide.region_13.14_spmd, body=%wide.region_10.13_spmd.sunk | while | flops 610656768 | bytes 29655648 | solution.py:91
  362.1 153.3 %all-gather.29.cloned.1.call-done = f32[8192,768]{1,0:T(8,128)} async-done(((f32[2048,768]{1,0:T(8,128)}), f32[8192,768]{1,0:T(8,128)}) %all-gather.29.cloned.1.call-update) | async-done | bytes 25165840 | tf_op jit(solution)/shard_map/all_gather | solution.py:183
  515.4 13.0 reduce_sum.392
  539.6 19.2 %multiply_convert_fusion.2 = (bf16[2048,768]{1,0:T(8,128)(2,1)}, f32[2048,768]{1,0:T(8,128)}, f32[2048,768]{1,0:T(8,128)}) fusion(bf16[2048,768]{1,0:T(8,128)(2,1)S(1)} %multiply_convert_fusion.3, bf16[768,768]{1,0:T(8,128)(2,1)} %all-gather.21.cloned.1.call-done), kind=kOutput, calls=%fused_computation.165 | convolution fusion | flops 2518155264 | bytes 20054016 | tf_op jit(solution)/shard_map/dot_general | solution.py:15
  563.8 7.7 fusion.146
  572.5 154.0 %all-gather.31.cloned.1.call-done = f32[8192,768]{1,0:T(8,128)} async-done(((f32[2048,768]{1,0:T(8,128)}), f32[8192,768]{1,0:T(8,128)}) %all-gather.31.cloned.1.call-update) | async-done | bytes 25165840 | tf_op jit(solution)/shard_map/all_gather | solution.py:183
  726.4 12.9 reduce_sum.448
  739.4 7.9 fusion.140
  747.3 9.2 all-gather.25.cloned.1.call-done
  766.0 7.1 add_convert_fusion
  779.4 154.9 %all-gather.33.cloned.1.call-done = f32[8192,768]{1,0:T(8,128)} async-done(((f32[2048,768]{1,0:T(8,128)}), f32[8192,768]{1,0:T(8,128)}) %all-gather.33.cloned.1.call-update) | async-done | bytes 25165840 | tf_op jit(solution)/shard_map/all_gather | solution.py:183
  934.3 12.6 reduce_sum.453
  969.5 110.9 %while.65 = (s32[]{:T(128)}, f32[1500,3,64]{0,2,1:T(8,128)S(1)}, f32[1500,3,64]{0,2,1:T(8,128)S(1)}, bf16[4,512,192]{1,2,0:T(8,128)(2,1)}, bf16[4,512,3,64]{1,3,...) while((s32[]{:T(128)}, f32[1500,3,64]{0,2,1:T(8,128)S(1)}, ...), condition=%wide.region_27.28_spmd.clone, body=%wide.region_25.27_spmd.clone.sunk | while | flops 1503843072 | bytes 135411952 | solution.py:134
  979.5 11.0 multiply_convert_fusion.8
  1007.2 11.0 multiply_convert_fusion.8
  1034.9 11.0 multiply_convert_fusion.8
  1062.6 11.0 multiply_convert_fusion.8
  1087.2 7.6 convolution_convert_fusion.8
  1117.9 124.3 %all-gather.35.cloned.1.call-done = f32[8192,768]{1,0:T(8,128)} async-done(((f32[2048,768]{1,0:T(8,128)}), f32[8192,768]{1,0:T(8,128)}) %all-gather.35.cloned.1.call-update) | async-done | bytes 25165840 | tf_op jit(solution)/shard_map/all_gather | solution.py:183
  1242.1 13.0 reduce_sum.456
  1261.7 6.0 fusion.137
  1281.8 142.4 %while.66 = (s32[]{:T(128)}, f32[2048,3,64]{0,2,1:T(8,128)}, f32[2048,3,64]{0,2,1:T(8,128)}, bf16[4,512,192]{1,2,0:T(8,128)(2,1)}, bf16[4,512,3,64]{1,3,2,0:T(8,...) while((s32[]{:T(128)}, f32[2048,3,64]{0,2,1:T(8,128)}, ...), condition=%wide.region_34.35_spmd.clone.clone, body=%wide.region_31.34_spmd.clone.clone.sunk | while | flops 2068954624 | bytes 147471712 | solution.py:134
  1294.8 5.8 multiply_reduce_fusion.24
  1300.6 6.1 multiply_convert_fusion.9
  1324.0 6.2 fusion.293
  1336.0 6.1 multiply_convert_fusion.9
  1360.1 6.2 fusion.293
  1372.0 6.1 multiply_convert_fusion.9
  1396.0 6.2 fusion.293
  1402.2 5.8 multiply_reduce_fusion.24
  1408.0 6.1 multiply_convert_fusion.9
  1439.6 6.6 convolution_convert_fusion.9
  1460.4 13.7 reduce-scatter.37.cloned.1.call-done
  1475.8 22.8 %reduce-scatter.31.cloned.1.call-done = bf16[384,768]{1,0:T(8,128)(2,1)} async-done(((bf16[768,768]{1,0:T(8,128)(2,1)}), bf16[384,768]{1,0:T(8,128)(2,1)}) %reduce-scatter.31.cloned.1.call-update) | async-done | bytes 589840 | tf_op jit(solution)/shard_map/reduce_scatter | solution.py:286
  1507.2 8.2 convert_element_type.265
  1525.0 25.6 %fusion.4 = bf16[376,768]{1,0:T(8,128)(2,1)} fusion(bf16[1500,768]{1,0:T(8,128)(2,1)} %add_convert_fusion.2), kind=kCustom, calls=%all-reduce-scatter | all-reduce-scatter fusion | flops 1155073 | bytes 2882048
  1565.6 31.9 %all-reduce.6.cloned.1.call-done = (bf16[384,192]{0,1:T(8,128)(2,1)}, bf16[384,192]{0,1:T(8,128)(2,1)}, bf16[384,192]{0,1:T(8,128)(2,1)}, bf16[192,384]{1,0:T(8,...) async-done(((bf16[384,192]{0,1:T(8,128)(2,1)}, ...) | async-done | bytes 2359312 | tf_op jit(solution)/shard_map/psum | solution.py:302
  1615.4 137.3 %all-gather.37.cloned.1.call-done = f32[8192,768]{1,0:T(8,128)} async-done(((f32[2048,768]{1,0:T(8,128)}), f32[8192,768]{1,0:T(8,128)}) %all-gather.37.cloned.1.call-update) | async-done | bytes 25165840 | tf_op jit(solution)/shard_map/all_gather | solution.py:183
  1752.7 12.6 reduce_sum.459
  1777.2 39.5 %all-reduce.2 = (f32[768]{0:T(1024)}, f32[768]{0:T(1024)}, f32[768]{0:T(1024)}, f32[768]{0:T(1024)}) all-reduce(f32[768]{0:T(1024)S(1)} %multiply_reduce_fusion.17, f32[768]{0:T(1024)S(1)} %multiply_reduce_fusion.15, f32[768]{0:T(1024)S(1)} %get-tuple-element.857, ...), channel_id=1, replica_groups=mesh['row'=4,'col'=2,'dp'=4] {'row','col','dp'}, use_global_device_ids=true, to_apply=%region_42.43 | all-reduce | flops 3072 | bytes 24576 | tf_op jit(solution)/shard_map/psum | solution.py:313
  (615 shorter events, 437.6 us)
Async XLA Ops:
  7.2 39.2 %copy-start.86 = (f32[768]{0:T(1024)S(1)}, f32[768]{0:T(1024)}, u32[]{:S(2)}) copy-start(f32[768]{0:T(1024)} %param.30) | copy-start | bytes 9220
  7.2 33.6 %all-gather.19.cloned.1.call-start = ((), (), s32[]{:S(2)}) async-start(), calls=%async_computation.10 | async-start | bytes 3932160 | tf_op jit(solution)/shard_map/all_gather | solution.py:169
  7.9 170.8 %all-gather.39.cloned.1.call-start = ((), (), s32[]{:S(2)}) async-start(), calls=%async_computation.21 | async-start | bytes 2887680 | tf_op jit(solution)/shard_map/all_gather | solution.py:169
  8.7 300.5 %all-gather.27.cloned.1.call-start = ((), (), s32[]{:S(2)}) async-start(), calls=%async_computation.15 | async-start | bytes 31457280 | tf_op jit(solution)/shard_map/all_gather | solution.py:183
  16.5 33.4 %copy-start.52 = (bf16[768,192]{0,1:T(8,128)(2,1)}, bf16[768,192]{0,1:T(8,128)(2,1)S(1)}, u32[]{:S(2)}) copy-start(bf16[768,192]{0,1:T(8,128)(2,1)S(1)} %all_gather.76) | copy-start | bytes 884740
  22.5 26.2 %copy-start.54 = (bf16[768,192]{0,1:T(8,128)(2,1)}, bf16[768,192]{0,1:T(8,128)(2,1)S(1)}, u32[]{:S(2)}) copy-start(bf16[768,192]{0,1:T(8,128)(2,1)S(1)} %all_gather.77) | copy-start | bytes 884740
  28.5 19.0 %copy-start.59 = (bf16[768,192]{0,1:T(8,128)(2,1)}, bf16[768,192]{0,1:T(8,128)(2,1)S(1)}, u32[]{:S(2)}) copy-start(bf16[768,192]{0,1:T(8,128)(2,1)S(1)} %all_gather.78) | copy-start | bytes 884740
  34.6 114.9 %copy-start.46 = (bf16[192,768]{1,0:T(8,128)(2,1)}, bf16[192,768]{1,0:T(8,128)(2,1)S(1)}, u32[]{:S(2)}) copy-start(bf16[192,768]{1,0:T(8,128)(2,1)S(1)} %all_gather.79) | copy-start | bytes 884740
  149.3 29.4 %copy-start.38 = (bf16[4,512,3,64]{1,3,2,0:T(8,128)(2,1)}, bf16[4,512,3,64]{1,3,2,0:T(8,128)(2,1)S(1)}, u32[]{:S(2)}) copy-start(bf16[4,512,3,64]{1,3,2,0:T(8,128)(2,1)S(1)} %get-tuple-element.1286) | copy-start | bytes 2359300
  149.3 172.5 %copy-start.68 = (f32[4,3,512]{2,1,0:T(4,128)}, f32[4,3,512]{2,1,0:T(4,128)S(1)}, u32[]{:S(2)}) copy-start(f32[4,3,512]{2,1,0:T(4,128)S(1)} %get-tuple-element.1179) | copy-start | bytes 73732
  150.5 10.6 copy-start.70
  154.2 12.7 copy-start.71
  154.2 18.5 %copy-start.72 = (bf16[192,384]{1,0:T(8,128)(2,1)S(1)}, bf16[192,384]{1,0:T(8,128)(2,1)}, u32[]{:S(2)}) copy-start(bf16[192,384]{1,0:T(8,128)(2,1)} %param.39) | copy-start | bytes 442372
  154.3 361.2 %all-gather.29.cloned.1.call-start = ((), (), s32[]{:S(2)}) async-start(), calls=%async_computation.16 | async-start | bytes 31457280 | tf_op jit(solution)/shard_map/all_gather | solution.py:183
  161.1 167.2 %copy-start.58 = (bf16[768,192]{0,1:T(8,128)(2,1)}, bf16[768,192]{0,1:T(8,128)(2,1)S(1)}, u32[]{:S(2)}) copy-start(bf16[768,192]{0,1:T(8,128)(2,1)S(1)} %all_gather.82) | copy-start | bytes 884740
  166.9 20.6 %copy-start.56 = (bf16[768,192]{0,1:T(8,128)(2,1)}, bf16[768,192]{0,1:T(8,128)(2,1)S(1)}, u32[]{:S(2)}) copy-start(bf16[768,192]{0,1:T(8,128)(2,1)S(1)} %all_gather.84) | copy-start | bytes 884740
  172.7 14.8 copy-start.61
  178.7 177.0 %copy-start.48 = (bf16[192,768]{1,0:T(8,128)(2,1)}, bf16[192,768]{1,0:T(8,128)(2,1)S(1)}, u32[]{:S(2)}) copy-start(bf16[192,768]{1,0:T(8,128)(2,1)S(1)} %all_gather.86) | copy-start | bytes 884740
  355.6 172.8 %copy-start.67 = (f32[4,3,512]{2,1,0:T(4,128)}, f32[4,3,512]{2,1,0:T(4,128)S(1)}, u32[]{:S(2)}) copy-start(f32[4,3,512]{2,1,0:T(4,128)S(1)} %get-tuple-element.1144) | copy-start | bytes 73732
  360.5 179.1 %all-gather.21.cloned.1.call-start = ((), (), s32[]{:S(2)}) async-start(), calls=%async_computation.11 | async-start | bytes 1769472 | tf_op jit(solution)/shard_map/all_gather | solution.py:195
  361.1 202.7 %all-gather.23.cloned.1.call-start = ((), (), s32[]{:S(2)}) async-start(), calls=%async_computation.12 | async-start | bytes 1769472 | tf_op jit(solution)/shard_map/all_gather | solution.py:200
  361.7 364.8 %all-gather.31.cloned.1.call-start = ((), (), s32[]{:S(2)}) async-start(), calls=%async_computation.17 | async-start | bytes 31457280 | tf_op jit(solution)/shard_map/all_gather | solution.py:183
  537.4 21.4 %copy-start.45 = (bf16[2048,768]{1,0:T(8,128)(2,1)}, bf16[2048,768]{1,0:T(8,128)(2,1)S(1)}, u32[]{:S(2)}) copy-start(bf16[2048,768]{1,0:T(8,128)(2,1)S(1)} %multiply_convert_fusion.3) | copy-start | bytes 9437188
  571.5 185.0 %all-gather.25.cloned.1.call-start = ((), (), s32[]{:S(2)}) async-start(), calls=%async_computation.13 | async-start | bytes 3932160 | tf_op jit(solution)/shard_map/all_gather | solution.py:169
  572.3 362.0 %all-gather.33.cloned.1.call-start = ((), (), s32[]{:S(2)}) async-start(), calls=%async_computation.18 | async-start | bytes 31457280 | tf_op jit(solution)/shard_map/all_gather | solution.py:183
  739.4 17.2 copy-start.84
  756.5 8.1 slice-start.12
  764.6 8.5 copy-start.23
  764.6 193.2 %copy-start.91 = (f32[2048]{0:T(1024)}, f32[2048]{0:T(1024)S(1)}, u32[]{:S(2)}) copy-start(f32[2048]{0:T(1024)S(1)} %negate_multiply_fusion.4) | copy-start | bytes 24580
  765.9 8.9 copy-start.94
  779.4 462.8 %all-gather.35.cloned.1.call-start = ((), (), s32[]{:S(2)}) async-start(), calls=%async_computation.19 | async-start | bytes 31457280 | tf_op jit(solution)/shard_map/all_gather | solution.py:183
  946.9 10.9 slice-start.10
  961.4 8.2 copy-start.7
  961.4 8.2 copy-start.27
  1087.2 359.1 %reduce-scatter.49.cloned.1.call-start = ((), (), s32[]{:S(2)}) async-start(), calls=%async_computation.30 | async-start | bytes 1769472
  1097.8 350.6 %reduce-scatter.47.cloned.1.call-start = ((), (), s32[]{:S(2)}) async-start(), calls=%async_computation.29 | async-start | bytes 589824
  1104.1 346.0 %reduce-scatter.41.cloned.1.call-start = ((), (), s32[]{:S(2)}) async-start(), calls=%async_computation.26 | async-start | bytes 589824
  1109.2 342.7 %reduce-scatter.43.cloned.1.call-start = ((), (), s32[]{:S(2)}) async-start(), calls=%async_computation.27 | async-start | bytes 589824
  1113.6 340.0 %reduce-scatter.45.cloned.1.call-start = ((), (), s32[]{:S(2)}) async-start(), calls=%async_computation.28 | async-start | bytes 589824
  1117.8 337.5 %reduce-scatter.39.cloned.1.call-start = ((), (), s32[]{:S(2)}) async-start(), calls=%async_computation.25 | async-start | bytes 589824
  1242.1 13.0 copy-start.66
  1242.1 13.0 copy-start.90
  1255.2 12.6 slice-start.4
  1280.8 176.1 %reduce-scatter.33.cloned.1.call-start = ((), (), s32[]{:S(2)}) async-start(), calls=%async_computation.22 | async-start | bytes 589824
  1282.0 8.0 copy-start.43
  1316.1 8.0 copy-start.43
  1352.1 8.0 copy-start.43
  1388.1 8.0 copy-start.43
  1430.1 28.6 %reduce-scatter.35.cloned.1.call-start = ((), (), s32[]{:S(2)}) async-start(), calls=%async_computation.23 | async-start | bytes 589824
  1435.2 38.9 %reduce-scatter.37.cloned.1.call-start = ((), (), s32[]{:S(2)}) async-start(), calls=%async_computation.24 | async-start | bytes 589824
  1439.5 59.2 %copy-start.37 = (bf16[2048,3,64]{0,2,1:T(8,128)(2,1)S(1)}, bf16[2048,3,64]{0,2,1:T(8,128)(2,1)}, u32[]{:S(2)}) copy-start(bf16[2048,3,64]{0,2,1:T(8,128)(2,1)} %copy-done.36) | copy-start | bytes 2359300
  1439.5 59.2 %copy-start.55 = (bf16[768,192]{0,1:T(8,128)(2,1)S(1)}, bf16[768,192]{0,1:T(8,128)(2,1)}, u32[]{:S(2)}) copy-start(bf16[768,192]{0,1:T(8,128)(2,1)} %copy-done.54) | copy-start | bytes 884740
  1439.5 59.1 %reduce-scatter.31.cloned.1.call-start = ((), (), s32[]{:S(2)}) async-start(), calls=%async_computation.14 | async-start | bytes 1769472 | tf_op jit(solution)/shard_map/reduce_scatter | solution.py:286
  1446.2 151.3 %all-reduce.6.cloned.1.call-start = ((), (), s32[]{:S(2)}) async-start(), calls=%async_computation.31 | async-start | bytes 4718592 | tf_op jit(solution)/shard_map/psum | solution.py:302
  1498.6 254.0 %all-gather.37.cloned.1.call-start = ((), (), s32[]{:S(2)}) async-start(), calls=%async_computation.20 | async-start | bytes 31457280 | tf_op jit(solution)/shard_map/all_gather | solution.py:183
  1506.6 9.3 slice-start
  1506.6 9.8 slice-start.2
  1507.1 8.7 copy-start.24
  1507.1 8.8 slice-start.1
  1507.1 9.7 slice-start.3
  1507.2 11.5 slice-start.8
  1551.3 5.0 collective-permute-start
  1752.7 14.9 copy-start.64
  1752.7 15.0 copy-start.87
  (96 other events, 377.0 us)
Sparse Core Ops, SparseCore 0:
  9.6 31.2 all-gather.18
  42.4 23.7 all-gather.38
  154.4 154.7 all-gather.26
  360.6 154.7 all-gather.28
  516.8 22.7 all-gather.20
  541.0 22.7 all-gather.22
  571.6 154.7 all-gather.30
  728.0 28.4 all-gather.24
  779.5 154.7 all-gather.32
  1087.3 154.7 all-gather.34
  1245.0 21.8 reduce-scatter.48
  1268.9 13.1 reduce-scatter.46
  1284.4 13.1 reduce-scatter.40
  1299.7 13.1 reduce-scatter.42
  1315.0 13.1 reduce-scatter.44
  1330.4 13.1 reduce-scatter.38
  1430.2 13.0 reduce-scatter.32
  1445.4 13.1 reduce-scatter.34
  1460.9 13.1 reduce-scatter.36
  1476.7 21.8 reduce-scatter.30
  1502.4 95.0 all-reduce.5
  1599.1 153.5 all-gather.36
